TPU v7x, 32 devices: a whole 2x2x4 slice. The times are simulated.
32 devices in a mesh: gx: 8 (over y, x, core), gy: 4 (over z).
Axes of the slice: x: 2, y: 2, z: 4, core: 2. Of those that a mesh axis runs over, the one named last changes fastest.
Arguments:
- density: float32 [32, 256, 256], P(('gx', 'gy')), may hold values from -0.06 to 0.56, as said below
- coupling: float32 [32, 256, 256], P(('gx', 'gy')), may hold values from -0.04 to 0.04
- weights: float32 [32], P(('gx', 'gy')), may hold values from 0.25 to 2
- live_mask: int32 [32], P(('gx', 'gy')), may hold values 0 or 1
- dimer_pairs: int32 [32, 2], replicated, may hold values from 0 to 31, as said below
- dimer_slot: int32 [32], replicated, may hold values from 0 to 31, as said below
- frag_slot: int32 [32], replicated, may hold values from 0 to 31, as said below
Outputs:
- refined: float32 [32, 256, 256], P(('gx', 'gy'))
Inputs may be any that keep to these rules, and one draw needn't show every extreme that they name: `dimer_slot`: each slot holds exactly one listed dimer. `frag_slot`: each fragment has its own slot; slot q lies on device q, devices numbered with gy fastest. `dimer_pairs`: the two fragments of a dimer differ. The dimers in slots k * 1 to (k + 1) - 1 (device k) name 2 fragments whose storage devices have pairwise different gx indices and pairwise different gy indices. `density`: each block is symmetric.
All inputs are finite; a program needn't handle non-finite values. No bound on the sum of `live_mask` on one device may be relied on, other than what follows from the above.
Results may differ from a plain program's by a relative error of at most 0.0003.
Values sent between devices are 32-bit elements; how exact they have to be, the bound alone decides.
A program may use at most 64 MiB of HBM per device.

v0:
```python
import functools
import jax
import jax.numpy as jnp
from jax import lax
from jax.experimental import pallas as pl
from jax.experimental.pallas import tpu as pltpu
from jax.sharding import PartitionSpec as P

ITERS = 3
MESH = pl.DeviceIdType.MESH
F32 = jnp.float32
BF16 = jnp.bfloat16


def split(value):
    high = value.astype(BF16)
    return high, (value - high.astype(F32)).astype(BF16)


def mm(left, right):
    return jnp.dot(left, right, preferred_element_type=F32)


def wrap(index, count):
    return jnp.where(index < 0, index + count, index)


def grid_iota(rows, columns):
    return (
        lax.broadcasted_iota(jnp.int32, (rows, columns), 0),
        lax.broadcasted_iota(jnp.int32, (rows, columns), 1),
    )


def kernel(
    count_x, count_y,
    density_in, coupling_in, weights_in, live_in, pairs_in, dslot_in, fslot_in,
    out_ref,
    density_ref, coupling_ref, weights_ref, live_ref, pairs_ref, dslot_ref, fslot_ref,
    codes, refs_s, packed, held, diag, held_diag, chosen, got, joined,
    matrix, m_high, m_low, q_high, q_low, square,
    grown, landed, extra, landed_extra, flat, table, totals, back,
    send_sems, recv_sems, stage_sems,
):
    count = count_x * count_y
    dim_dev = coupling_ref.shape[0]
    refs = 2 * dim_dev
    dimers = dslot_ref.shape[0]
    width = density_ref.shape[1]
    half = width // 2
    rows = width // count
    me = lax.axis_index("gx") * count_y + lax.axis_index("gy")

    def peer(step):
        other = lax.rem(me + step, count)
        return other, (lax.div(other, count_y), lax.rem(other, count_y))

    barrier = pltpu.get_barrier_semaphore()

    def greet(step, carry):
        pl.semaphore_signal(barrier, inc=1, device_id=peer(step)[1], device_id_type=MESH)
        return carry

    lax.fori_loop(1, count, greet, 0)

    staged = [
        pltpu.make_async_copy(source, target, stage_sems.at[place])
        for place, (source, target) in enumerate((
            (density_in, density_ref), (dslot_in, dslot_ref), (fslot_in, fslot_ref),
            (pairs_in, pairs_ref), (weights_in, weights_ref), (live_in, live_ref),
            (coupling_in, coupling_ref),
        ))
    ]
    for copy in staged:
        copy.start()
    staged[0].wait()

    row_id, column_id = grid_iota(half, half)
    upper = row_id <= column_id
    strict = row_id > column_id
    on_diag = row_id == column_id

    def pack(first, corner, second):
        mixed = jnp.where(upper, first, second)
        return corner, mixed, jnp.sum(jnp.where(on_diag, second, 0.0), axis=0, keepdims=True)

    def scatter_rows(target, corner, mixed):
        for piece in range(count):
            start = piece * rows
            source = corner if start < half else mixed
            start = start % half
            target(piece, source[start:start + rows])

    corner, mixed, diag_row = pack(
        density_ref[0, :half, :half], density_ref[0, :half, half:], density_ref[0, half:, half:]
    )

    def put_packed(piece, value):
        packed[piece] = value

    scatter_rows(put_packed, corner, mixed)
    diag[...] = diag_row

    pl.semaphore_wait(barrier, count - 1)

    def exchange(phase, source, target, same):
        def send(turn, carry, lag):
            step = turn * count_y + lag
            other, where_to = peer(step)
            pltpu.make_async_remote_copy(
                src_ref=source if same else source.at[other],
                dst_ref=target.at[count - step],
                send_sem=send_sems.at[phase],
                recv_sem=recv_sems.at[phase],
                device_id=where_to,
                device_id_type=MESH,
            ).start()
            return carry

        for lag in sorted(range(count_y), key=lambda lag: -min(lag, count_y - lag)):
            lax.fori_loop(
                0 if lag else 1, count_x, functools.partial(send, lag=lag), 0, unroll=count_x <= 8
            )

    def wait_for(sems, phase, target):
        span = target.at[pl.ds(1, count - 1)]
        pltpu.make_async_copy(span, span, sems.at[phase]).wait()

    exchange(0, packed, held, False)
    exchange(1, diag, held_diag, True)
    held[0] = packed[me]
    held_diag[0] = diag[...]

    for copy in staged[1:]:
        copy.wait()

    def code_of(dimer, carry):
        codes[dimer] = fslot_ref[pairs_ref[0, dimer]] * count + fslot_ref[pairs_ref[1, dimer]]
        return carry

    lax.fori_loop(0, dimers, code_of, 0)

    def names(slot, carry):
        def look(dimer, found):
            return jnp.where(dslot_ref[dimer] == slot, codes[dimer], found)

        found = lax.fori_loop(0, dimers, look, jnp.int32(0), unroll=dimers <= 64)
        refs_s[2 * slot] = lax.div(found, jnp.int32(count))
        refs_s[2 * slot + 1] = lax.rem(found, jnp.int32(count))
        return carry

    lax.fori_loop(0, count * dim_dev, names, 0)

    wait_for(recv_sems, 0, held)

    def choose(target, carry):
        for ref in range(refs):
            slot = refs_s[target * refs + ref]
            chosen[target, ref] = held[wrap(slot - me, count)]
        return carry

    lax.fori_loop(0, count, choose, 0, unroll=count <= 32)
    exchange(2, chosen, got, False)
    got[0] = chosen[me]
    wait_for(recv_sems, 1, held_diag)

    lanes = count * refs * rows
    lane_id = lax.broadcasted_iota(jnp.int32, (1, lanes), 1)
    lane_ref = lane_id // rows

    def spread(entry, row):
        ref = lax.rem(entry, refs)
        source = lax.rem(me + lax.div(entry, refs), count)
        return jnp.where(lane_ref == entry, refs_s[source * refs + ref], row)

    named = lax.fori_loop(
        0, count * refs, spread, jnp.zeros((1, lanes), jnp.int32), unroll=count * refs <= 64
    )
    named = named * rows + lane_id % rows
    table_row = lax.broadcasted_iota(jnp.int32, (count * rows, lanes), 0)
    table[...] = jnp.where(table_row == named, 1.0, 0.0).astype(BF16)

    def couple(dimer):
        coupled = coupling_ref[dimer]
        matrix[:width, width:] = coupled
        matrix[width:, :width] = coupled.T

    couple(0)
    wait_for(recv_sems, 2, got)

    for dimer in range(dim_dev):
        if dimer:
            couple(dimer)
        for side in range(2):
            ref = 2 * dimer + side
            for piece in range(count):
                joined[piece * rows:(piece + 1) * rows, :] = got[wrap(piece - me, count), ref]
            corner = joined[:half, :]
            mixed = joined[half:, :]
            turned = mixed.T
            slot = refs_s[me * refs + ref]
            diag_row = held_diag[wrap(slot - me, count)]
            low = side * width
            mid = low + half
            high = low + width
            matrix[low:mid, low:mid] = jnp.where(upper, mixed, turned)
            matrix[low:mid, mid:high] = corner
            matrix[mid:high, low:mid] = corner.T
            matrix[mid:high, mid:high] = jnp.where(
                on_diag, diag_row, jnp.where(strict, mixed, turned)
            )
        for repeat in range(ITERS):
            m_high[...], m_low[...] = split(matrix[...])
            square[...] = (
                mm(m_high[...], m_high[...])
                + mm(m_high[...], m_low[...])
                + mm(m_low[...], m_high[...])
            )
            q_high[...], q_low[...] = split(square[...])
            if repeat < ITERS - 1:
                cuts = ((slice(None), slice(None)),)
            else:
                cuts = tuple(
                    (slice(side * width, (side + 1) * width),) * 2 for side in range(2)
                )
            for across, down in cuts:
                cube = (
                    mm(q_high[across, :], m_high[:, down])
                    + mm(q_high[across, :], m_low[:, down])
                    + mm(q_low[across, :], m_high[:, down])
                )
                matrix[across, down] = 3.0 * square[across, down] - 2.0 * cube
        factor = jnp.where(live_ref[dimer] > 0, weights_ref[dimer], jnp.float32(0.0))
        for side in range(2):
            ref = 2 * dimer + side
            low = side * width
            mid = low + half
            high = low + width
            corner, mixed, diag_row = pack(
                factor * matrix[low:mid, low:mid],
                factor * matrix[low:mid, mid:high],
                factor * matrix[mid:high, mid:high],
            )

            def put_grown(piece, value, ref=ref):
                grown[piece, ref] = value

            scatter_rows(put_grown, corner, mixed)
            extra[ref:ref + 1, :] = diag_row
            extra[refs + ref:refs + ref + 1, :] = jnp.full((1, half), factor, F32)

    exchange(3, grown, landed, False)
    exchange(4, extra, landed_extra, True)
    landed[0] = grown[me]
    landed_extra[0] = extra[...]

    wait_for(recv_sems, 3, landed)
    if rows == 8:
        values = landed[...].reshape(lanes, half)
    else:
        for entry in range(count * refs):
            flat[entry * rows:(entry + 1) * rows, :] = landed[entry // refs, entry % refs]
        values = flat[...]
    first, rest = values.astype(BF16), None
    rest = values - first.astype(F32)
    second, third = split(rest)
    sums = mm(table[...], first) + mm(table[...], second) + mm(table[...], third)
    for piece in range(count):
        totals[piece] = sums[piece * rows:(piece + 1) * rows, :]
    exchange(5, totals, back, False)
    back[0] = totals[me]

    wait_for(recv_sems, 4, landed_extra)
    which = lax.broadcasted_iota(jnp.int32, (2 * refs, half), 0) % refs

    def collect(entry, carry):
        source = lax.rem(me + entry, count)
        mask = jnp.zeros((2 * refs, half), jnp.int32)
        for ref in range(refs):
            hit = jnp.where(refs_s[source * refs + ref] == me, 1, 0)
            mask = jnp.where(which == ref, hit, mask)
        return carry + jnp.where(mask > 0, landed_extra[entry], 0.0)

    side_sums = lax.fori_loop(
        0, count, collect, jnp.zeros((2 * refs, half), F32), unroll=count <= 32
    )
    diag_total = jnp.sum(side_sums[:refs], axis=0, keepdims=True)
    scale = 1.0 + jnp.sum(side_sums[refs:], axis=0, keepdims=True)

    wait_for(recv_sems, 5, back)
    for piece in range(count):
        joined[piece * rows:(piece + 1) * rows, :] = back[wrap(piece - me, count)]
    corner = joined[:half, :]
    mixed = joined[half:, :]
    turned = mixed.T
    out_ref[0, :half, :half] = (
        density_ref[0, :half, :half] + jnp.where(upper, mixed, turned)
    ) / scale
    out_ref[0, :half, half:] = (density_ref[0, :half, half:] + corner) / scale
    out_ref[0, half:, :half] = (density_ref[0, half:, :half] + corner.T) / scale
    out_ref[0, half:, half:] = (
        density_ref[0, half:, half:]
        + jnp.where(on_diag, diag_total, jnp.where(strict, mixed, turned))
    ) / scale

    for phase, target in enumerate((held, held_diag, got, landed, landed_extra, back)):
        wait_for(send_sems, phase, target)


def solution(mesh):
    count_x, count_y = mesh.shape["gx"], mesh.shape["gy"]
    count = count_x * count_y

    def per_device(density, coupling, weights, live_mask, dimer_pairs, dimer_slot, frag_slot):
        frag_dev, width, _ = density.shape
        dim_dev = coupling.shape[0]
        refs = 2 * dim_dev
        half = width // 2
        rows = width // count
        assert frag_dev == 1 and rows * count == width
        vmem = lambda *shape: pltpu.VMEM(shape, F32)
        bf16 = lambda *shape: pltpu.VMEM(shape, BF16)
        in_vmem = pl.BlockSpec(memory_space=pltpu.VMEM)
        smem = lambda array: pltpu.SMEM(array.shape, array.dtype)
        pairs = dimer_pairs.T
        return pl.pallas_call(
            functools.partial(kernel, count_x, count_y),
            out_shape=pltpu.VMEM(density.shape, F32),
            in_specs=[pl.BlockSpec(memory_space=pl.ANY)] * 7,
            out_specs=in_vmem,
            scratch_shapes=[
                vmem(*density.shape),
                vmem(*coupling.shape),
                smem(weights),
                smem(live_mask),
                smem(pairs),
                smem(dimer_slot),
                smem(frag_slot),
                pltpu.SMEM((dimer_slot.shape[0],), jnp.int32),
                pltpu.SMEM((count * refs,), jnp.int32),
                vmem(count, rows, half),
                vmem(count, rows, half),
                vmem(1, half),
                vmem(count, 1, half),
                vmem(count, refs, rows, half),
                vmem(count, refs, rows, half),
                vmem(width, half),
                vmem(2 * width, 2 * width),
                bf16(2 * width, 2 * width),
                bf16(2 * width, 2 * width),
                bf16(2 * width, 2 * width),
                bf16(2 * width, 2 * width),
                vmem(2 * width, 2 * width),
                vmem(count, refs, rows, half),
                vmem(count, refs, rows, half),
                vmem(2 * refs, half),
                vmem(count, 2 * refs, half),
                vmem(count * refs * rows if rows != 8 else 8, half),
                bf16(count * rows, count * refs * rows),
                vmem(count, rows, half),
                vmem(count, rows, half),
                pltpu.SemaphoreType.DMA((6,)),
                pltpu.SemaphoreType.DMA((6,)),
                pltpu.SemaphoreType.DMA((7,)),
            ],
            compiler_params=pltpu.CompilerParams(collective_id=0, has_side_effects=True),
        )(density, coupling, weights, live_mask, pairs, dimer_slot, frag_slot)

    both = ("gx", "gy")
    return jax.shard_map(
        per_device,
        mesh=mesh,
        in_specs=(
            P(both, None, None),
            P(both, None, None),
            P(both),
            P(both),
            P(),
            P(),
            P(),
        ),
        out_specs=P(both, None, None),
        check_vma=False,
    )
```

profile of v0, /device:TPU:0, one launch (start us, length us, event | category | flops | bytes accessed | tf_op | source)
XLA Modules:
  0.0 41.1 jit_solution(3541559275811659712)
XLA Ops:
  1.3 39.1 %shard_map.73 = f32[1,256,256]{2,1,0:T(8,128)S(1)} custom-call(f32[1,256,256]{2,1,0:T(8,128)} %density_in.1, f32[1,256,256]{2,1,0:T(8,128)} %coupling_in.1, f32[1]{0:T(128)S(6)} %copy.10.weights_in, s32[1]{0:T(128)S(6)} %copy.11.live_in, s32[2,32]{1,0:T(2,128)} %bitcast.1, s32[32]{0:T(128)} %dslot_in.1, s32[32]{0:T(128)} %fslot_in.1), custom_call_target="tpu_custom_call" | custom-call | tf_op jit(solution)/shard_map/pallas_call | solution.py:326
  40.4 0.7 %copy.9 = f32[1,256,256]{2,1,0:T(8,128)} copy(f32[1,256,256]{2,1,0:T(8,128)S(1)} %shard_map.73) | data formatting | bytes 524288
where the time goes:
time: 41.3 us; the launch traced here: 41.1 us
  Pallas kernels  39.1 us (95%)
  between operations  1.3 us (3%)
  local copies, waits for them, and re-layouts  0.71 us (2%)
    pallas_call x1, Pallas kernels, per_device(): pl.pallas_call(functools.partial(kernel, count_x, count_y), out_shape=plt...  39.1 us

commit v1 on v0

v1 whole, which is shorter than its diff:
```python
import functools
import jax
import jax.numpy as jnp
from jax import lax
from jax.experimental import pallas as pl
from jax.experimental.pallas import tpu as pltpu
from jax.sharding import PartitionSpec as P

ITERS = 3
MESH = pl.DeviceIdType.MESH
F32 = jnp.float32
BF16 = jnp.bfloat16


def split(value):
    high = value.astype(BF16)
    return high, (value - high.astype(F32)).astype(BF16)


def mm(left, right):
    return jnp.dot(left, right, preferred_element_type=F32)


def wrap(index, count):
    return jnp.where(index < 0, index + count, index)


def grid_iota(rows, columns):
    return (
        lax.broadcasted_iota(jnp.int32, (rows, columns), 0),
        lax.broadcasted_iota(jnp.int32, (rows, columns), 1),
    )


def kernel(
    count_x, count_y,
    density_in, coupling_in, weights_in, live_in, pairs_in, dslot_in, fslot_in,
    out_ref,
    density_ref, coupling_ref, weights_ref, live_ref, pairs_ref, dslot_ref, fslot_ref,
    codes, refs_s, packed, held, note, held_note, chosen, got, joined,
    m_high, m_low, q_high, q_low, square,
    grown, landed, extra, landed_extra, flat, table, totals, back,
    send_sems, recv_sems, stage_sems,
):
    count = count_x * count_y
    dim_dev = coupling_ref.shape[0]
    refs = 2 * dim_dev
    dimers = dslot_ref.shape[0]
    width = density_ref.shape[1]
    half = width // 2
    near_y = count_y // 2
    team = count_x * near_y
    rows = width // team
    my_x, my_y = lax.axis_index("gx"), lax.axis_index("gy")
    me = my_x * count_y + my_y
    my_seat = my_x * near_y + lax.rem(my_y, near_y)
    first_y = my_y - lax.rem(my_y, near_y)
    spread_at, note_at, chosen_at = 0, 1, 2
    grown_at = chosen_at + 1
    extra_at = grown_at + refs
    total_at = extra_at + 1

    def peer(step):
        other = lax.rem(me + step, count)
        return other, (lax.div(other, count_y), lax.rem(other, count_y))

    def mate(step):
        seat = lax.rem(my_seat + step, team)
        x, y = lax.div(seat, near_y), first_y + lax.rem(seat, near_y)
        return x * count_y + y, (x, y)

    def seat_of(device):
        return lax.div(device, count_y) * near_y + lax.rem(lax.rem(device, count_y), near_y)

    barrier = pltpu.get_barrier_semaphore()

    def greet(step, carry):
        pl.semaphore_signal(barrier, inc=1, device_id=peer(step)[1], device_id_type=MESH)
        return carry

    lax.fori_loop(1, count, greet, 0)

    staged = [
        pltpu.make_async_copy(source, target, stage_sems.at[place])
        for place, (source, target) in enumerate((
            (density_in, density_ref), (dslot_in, dslot_ref), (fslot_in, fslot_ref),
            (pairs_in, pairs_ref), (weights_in, weights_ref), (live_in, live_ref),
            (coupling_in, coupling_ref),
        ))
    ]
    for copy in staged:
        copy.start()
    staged[0].wait()

    row_id, column_id = grid_iota(half, half)
    upper = row_id <= column_id
    strict = row_id > column_id
    on_diag = row_id == column_id

    def pack(first, corner, second):
        mixed = jnp.where(upper, first, second)
        return corner, mixed, jnp.sum(jnp.where(on_diag, second, 0.0), axis=0, keepdims=True)

    def scatter_rows(target, corner, mixed):
        for piece in range(team):
            start = piece * rows
            source = corner if start < half else mixed
            start = start % half
            target[piece] = source[start:start + rows]

    def factor_of(dimer):
        return jnp.where(live_ref[dimer] > 0, weights_ref[dimer], jnp.float32(0.0))

    corner, mixed, diag_row = pack(
        density_ref[0, :half, :half], density_ref[0, :half, half:], density_ref[0, half:, half:]
    )
    scatter_rows(packed, corner, mixed)
    for copy in staged[4:6]:
        copy.wait()
    note[0:1, :] = diag_row
    for dimer in range(dim_dev):
        note[dimer + 1:dimer + 2, :] = jnp.full((1, half), factor_of(dimer), F32)

    pl.semaphore_wait(barrier, count - 1)

    def push(phase, source, target, where_to):
        pltpu.make_async_remote_copy(
            src_ref=source,
            dst_ref=target,
            send_sem=send_sems.at[phase],
            recv_sem=recv_sems.at[phase],
            device_id=where_to,
            device_id_type=MESH,
        ).start()

    def visit(act, cycle):
        def at(turn, carry, lag):
            act(turn * cycle + lag)
            return carry

        for lag in sorted(range(cycle), key=lambda lag: -min(lag, cycle - lag)):
            lax.fori_loop(
                0 if lag else 1, count_x, functools.partial(at, lag=lag), 0, unroll=count_x <= 8
            )

    def to_all(phase, piece_for, target):
        def act(step):
            other, where_to = peer(step)
            push(phase, piece_for(other), target.at[count - step], where_to)

        visit(act, count_y)

    def to_team(phase, piece_for, target):
        def act(step):
            other, where_to = mate(step)
            push(phase, piece_for(other), target.at[team - step], where_to)

        visit(act, near_y)

    def drain(sems, phase, target, number):
        span = target.at[pl.ds(1, number - 1)]
        pltpu.make_async_copy(span, span, sems.at[phase]).wait()

    to_all(spread_at, lambda other: packed.at[seat_of(other)], held)
    to_all(note_at, lambda other: note, held_note)
    held[0] = packed[my_seat]
    held_note[0] = note[...]

    for copy in staged[1:4] + staged[6:]:
        copy.wait()

    def code_of(dimer, carry):
        codes[dimer] = fslot_ref[pairs_ref[0, dimer]] * count + fslot_ref[pairs_ref[1, dimer]]
        return carry

    lax.fori_loop(0, dimers, code_of, 0)

    def names(slot, carry):
        def look(dimer, found):
            return jnp.where(dslot_ref[dimer] == slot, codes[dimer], found)

        found = lax.fori_loop(0, dimers, look, jnp.int32(0), unroll=dimers <= 64)
        refs_s[2 * slot] = lax.div(found, jnp.int32(count))
        refs_s[2 * slot + 1] = lax.rem(found, jnp.int32(count))
        return carry

    lax.fori_loop(0, count * dim_dev, names, 0)

    drain(recv_sems, spread_at, held, count)

    def choose(seat, carry):
        target = lax.div(seat, near_y) * count_y + first_y + lax.rem(seat, near_y)
        for ref in range(refs):
            slot = refs_s[target * refs + ref]
            chosen[seat, ref] = held[wrap(slot - me, count)]
        return carry

    lax.fori_loop(0, team, choose, 0, unroll=team <= 32)
    to_team(chosen_at, lambda other: chosen.at[seat_of(other)], got)
    got[0] = chosen[my_seat]

    span = team * rows
    lanes = refs * span
    lane_id = lax.broadcasted_iota(jnp.int32, (1, lanes), 1)
    lane_entry = lane_id // rows

    def spread(entry, row):
        ref = lax.div(entry, team)
        source = mate(lax.rem(entry, team))[0]
        return jnp.where(lane_entry == entry, refs_s[source * refs + ref], row)

    named = lax.fori_loop(
        0, team * refs, spread, jnp.zeros((1, lanes), jnp.int32), unroll=team * refs <= 64
    )
    named = named * rows + lane_id % rows
    table_row = lax.broadcasted_iota(jnp.int32, (count * rows, lanes), 0)
    table[...] = jnp.where(table_row == named, 1.0, 0.0).astype(BF16)

    top, low = slice(0, width), slice(width, 2 * width)
    every = slice(0, 2 * width)

    def put(across, down, value):
        m_high[across, down], m_low[across, down] = split(value)

    def keep(across, down, value):
        square[across, down] = value
        q_high[across, down], q_low[across, down] = split(value)

    def times(left, across, middle, right, down):
        high, rest = left
        high_right, rest_right = right
        return (
            mm(high[across, middle], high_right[middle, down])
            + mm(high[across, middle], rest_right[middle, down])
            + mm(rest[across, middle], high_right[middle, down])
        )

    m_pair, q_pair = (m_high, m_low), (q_high, q_low)

    def couple(dimer):
        coupled = coupling_ref[dimer]
        put(top, low, coupled)
        put(low, top, coupled.T)
        square[top, top] = times(m_pair, top, low, m_pair, top)
        square[low, low] = times(m_pair, low, top, m_pair, low)

    def place(ref, side):
        for piece in range(team):
            joined[piece * rows:(piece + 1) * rows, :] = got[wrap(piece - my_seat, team), ref]
        corner = joined[:half, :]
        mixed = joined[half:, :]
        turned = mixed.T
        slot = refs_s[me * refs + ref]
        diag_row = held_note[wrap(slot - me, count), 0:1, :]
        start = side * width
        mid = start + half
        end = start + width
        put(slice(start, mid), slice(start, mid), jnp.where(upper, mixed, turned))
        put(slice(start, mid), slice(mid, end), corner)
        put(slice(mid, end), slice(start, mid), corner.T)
        put(
            slice(mid, end), slice(mid, end),
            jnp.where(on_diag, diag_row, jnp.where(strict, mixed, turned)),
        )

    def emit(ref, block):
        corner, mixed, diag_row = pack(block[:half, :half], block[:half, half:], block[half:, half:])
        scatter_rows(grown.at[ref], corner, mixed)
        extra[ref:ref + 1, :] = diag_row
        to_team(grown_at + ref, lambda other: grown.at[ref, seat_of(other)], landed.at[ref])

    couple(0)
    drain(recv_sems, note_at, held_note, count)
    drain(recv_sems, chosen_at, got, team)

    for dimer in range(dim_dev):
        first, second = 2 * dimer, 2 * dimer + 1
        factor = factor_of(dimer)
        if dimer:
            couple(dimer)
        place(first, 0)
        keep(top, top, square[top, top] + times(m_pair, top, top, m_pair, top))
        square[top, low] = times(m_pair, top, top, m_pair, low)
        place(second, 1)
        keep(top, low, square[top, low] + times(m_pair, top, low, m_pair, low))
        keep(low, low, square[low, low] + times(m_pair, low, low, m_pair, low))
        for repeat in range(ITERS - 1):
            across = 3.0 * square[top, low] - 2.0 * times(q_pair, top, every, m_pair, low)
            upper_left = 3.0 * square[top, top] - 2.0 * times(q_pair, top, every, m_pair, top)
            lower_right = 3.0 * square[low, low] - 2.0 * times(m_pair, low, every, q_pair, low)
            put(top, low, across)
            put(low, top, across.T)
            put(top, top, upper_left)
            put(low, low, lower_right)
            keep(top, top, times(m_pair, top, every, m_pair, top))
            keep(top, low, times(m_pair, top, every, m_pair, low))
            if repeat < ITERS - 2:
                keep(low, low, times(m_pair, low, every, m_pair, low))
        emit(first, factor * (
            3.0 * square[top, top] - 2.0 * times(q_pair, top, every, m_pair, top)
        ))
        keep(low, low, times(m_pair, low, every, m_pair, low))
        emit(second, factor * (
            3.0 * square[low, low] - 2.0 * times(m_pair, low, every, q_pair, low)
        ))

    to_all(extra_at, lambda other: extra, landed_extra)
    for ref in range(refs):
        landed[ref, 0] = grown[ref, my_seat]
    landed_extra[0] = extra[...]

    for ref in range(refs):
        drain(recv_sems, grown_at + ref, landed.at[ref], team)
        if rows % 8 == 0:
            values = landed[ref].reshape(span, half)
        else:
            for entry in range(team):
                flat[entry * rows:(entry + 1) * rows, :] = landed[ref, entry]
            values = flat[...]
        gained = mm(table[:, ref * span:(ref + 1) * span], jnp.concatenate(split(values), axis=1))
        gained = gained[:, :half] + gained[:, half:]
        sums = gained if ref == 0 else sums + gained
    for piece in range(count):
        totals[piece] = sums[piece * rows:(piece + 1) * rows, :]
    to_all(total_at, lambda other: totals.at[other], back)
    back[0] = totals[me]

    drain(recv_sems, extra_at, landed_extra, count)

    def collect(entry, carry):
        source = lax.rem(me + entry, count)
        diag_total, scale = carry
        for ref in range(refs):
            hit = jnp.where(refs_s[source * refs + ref] == me, 1, 0)
            mask = jnp.full((1, half), hit, jnp.int32) > 0
            diag_total = diag_total + jnp.where(mask, landed_extra[entry, ref:ref + 1, :], 0.0)
            row = 1 + ref // 2
            scale = scale + jnp.where(mask, held_note[entry, row:row + 1, :], 0.0)
        return diag_total, scale

    diag_total, scale = lax.fori_loop(
        0, count, collect, (jnp.zeros((1, half), F32), jnp.ones((1, half), F32)),
        unroll=count <= 32,
    )

    drain(recv_sems, total_at, back, count)
    for piece in range(team):
        source = piece // near_y * count_y + piece % near_y
        joined[piece * rows:(piece + 1) * rows, :] = (
            back[wrap(source - me, count)] + back[wrap(source + near_y - me, count)]
        )
    corner = joined[:half, :]
    mixed = joined[half:, :]
    turned = mixed.T
    out_ref[0, :half, :half] = (
        density_ref[0, :half, :half] + jnp.where(upper, mixed, turned)
    ) / scale
    out_ref[0, :half, half:] = (density_ref[0, :half, half:] + corner) / scale
    out_ref[0, half:, :half] = (density_ref[0, half:, :half] + corner.T) / scale
    out_ref[0, half:, half:] = (
        density_ref[0, half:, half:]
        + jnp.where(on_diag, diag_total, jnp.where(strict, mixed, turned))
    ) / scale

    drain(send_sems, spread_at, held, count)
    drain(send_sems, note_at, held_note, count)
    drain(send_sems, chosen_at, got, team)
    for ref in range(refs):
        drain(send_sems, grown_at + ref, landed.at[ref], team)
    drain(send_sems, extra_at, landed_extra, count)
    drain(send_sems, total_at, back, count)


def solution(mesh):
    count_x, count_y = mesh.shape["gx"], mesh.shape["gy"]
    count = count_x * count_y

    def per_device(density, coupling, weights, live_mask, dimer_pairs, dimer_slot, frag_slot):
        frag_dev, width, _ = density.shape
        dim_dev = coupling.shape[0]
        refs = 2 * dim_dev
        half = width // 2
        team = count // 2
        rows = width // team
        assert frag_dev == 1 and rows * team == width and count_y % 2 == 0
        vmem = lambda *shape: pltpu.VMEM(shape, F32)
        bf16 = lambda *shape: pltpu.VMEM(shape, BF16)
        in_vmem = pl.BlockSpec(memory_space=pltpu.VMEM)
        smem = lambda array: pltpu.SMEM(array.shape, array.dtype)
        pairs = dimer_pairs.T
        phases = 5 + refs
        return pl.pallas_call(
            functools.partial(kernel, count_x, count_y),
            out_shape=pltpu.VMEM(density.shape, F32),
            in_specs=[pl.BlockSpec(memory_space=pl.ANY)] * 7,
            out_specs=in_vmem,
            scratch_shapes=[
                vmem(*density.shape),
                vmem(*coupling.shape),
                smem(weights),
                smem(live_mask),
                smem(pairs),
                smem(dimer_slot),
                smem(frag_slot),
                pltpu.SMEM((dimer_slot.shape[0],), jnp.int32),
                pltpu.SMEM((count * refs,), jnp.int32),
                vmem(team, rows, half),
                vmem(count, rows, half),
                vmem(1 + dim_dev, half),
                vmem(count, 1 + dim_dev, half),
                vmem(team, refs, rows, half),
                vmem(team, refs, rows, half),
                vmem(width, half),
                bf16(2 * width, 2 * width),
                bf16(2 * width, 2 * width),
                bf16(2 * width, 2 * width),
                bf16(2 * width, 2 * width),
                vmem(2 * width, 2 * width),
                vmem(refs, team, rows, half),
                vmem(refs, team, rows, half),
                vmem(refs, half),
                vmem(count, refs, half),
                vmem(team * rows if rows % 8 else 8, half),
                bf16(count * rows, refs * team * rows),
                vmem(count, rows, half),
                vmem(count, rows, half),
                pltpu.SemaphoreType.DMA((phases,)),
                pltpu.SemaphoreType.DMA((phases,)),
                pltpu.SemaphoreType.DMA((7,)),
            ],
            compiler_params=pltpu.CompilerParams(collective_id=0, has_side_effects=True),
        )(density, coupling, weights, live_mask, pairs, dimer_slot, frag_slot)

    both = ("gx", "gy")
    return jax.shard_map(
        per_device,
        mesh=mesh,
        in_specs=(
            P(both, None, None),
            P(both, None, None),
            P(both),
            P(both),
            P(),
            P(),
            P(),
        ),
        out_specs=P(both, None, None),
        check_vma=False,
    )
```

time: 41.3 us -> 40.1 us (0.971)
  Pallas kernels: 39.1 us -> 37.9 us
    pallas_call x1, Pallas kernels: 39.1 us -> 37.9 us  [per_device(): pl.pallas_call(functools.partial(kernel, count_x, count_y), out_shape=plt...]
where the time goes in v1:
time: 40.1 us; the launch traced here: 40 us
  Pallas kernels  37.9 us (95%)
  between operations  1.3 us (3%)
  local copies, waits for them, and re-layouts  0.71 us (2%)
    pallas_call x1, Pallas kernels, per_device(): pl.pallas_call(functools.partial(kernel, count_x, count_y), out_shape=plt...  37.9 us

profile of v1, /device:TPU:0, one launch (start us, length us, event | category | flops | bytes accessed | tf_op | source)
XLA Modules:
  0.0 40.0 jit_solution(8354625499383283922)
XLA Ops:
  1.3 37.9 %shard_map.73 = f32[1,256,256]{2,1,0:T(8,128)S(1)} custom-call(f32[1,256,256]{2,1,0:T(8,128)} %density_in.1, f32[1,256,256]{2,1,0:T(8,128)} %coupling_in.1, f32[1]{0:T(128)S(6)} %copy.10.weights_in, s32[1]{0:T(128)S(6)} %copy.11.live_in, s32[2,32]{1,0:T(2,128)} %bitcast.1, s32[32]{0:T(128)} %dslot_in.1, s32[32]{0:T(128)} %fslot_in.1), custom_call_target="tpu_custom_call" | custom-call | tf_op jit(solution)/shard_map/pallas_call | solution.py:392
  39.2 0.7 %copy.9 = f32[1,256,256]{2,1,0:T(8,128)} copy(f32[1,256,256]{2,1,0:T(8,128)S(1)} %shard_map.73) | data formatting | bytes 524288

commit v2 on v1

--- a/solution.py
+++ b/solution.py
@@ -37,10 +37,10 @@
     density_in, coupling_in, weights_in, live_in, pairs_in, dslot_in, fslot_in,
     out_ref,
     density_ref, coupling_ref, weights_ref, live_ref, pairs_ref, dslot_ref, fslot_ref,
-    codes, refs_s, packed, held, note, held_note, chosen, got, joined,
+    codes, refs_s, packed, held, note, held_note, notice, mine, chosen, got, joined,
     m_high, m_low, q_high, q_low, square,
-    grown, landed, extra, landed_extra, flat, table, totals, back,
-    send_sems, recv_sems, stage_sems,
+    grown_first, grown_second, landed_first, landed_second, flat, table, totals, back, cross, crossed,
+    send_sems, recv_sems, stage_sems, ready,
 ):
     count = count_x * count_y
     dim_dev = coupling_ref.shape[0]
@@ -55,10 +55,9 @@
     me = my_x * count_y + my_y
     my_seat = my_x * near_y + lax.rem(my_y, near_y)
     first_y = my_y - lax.rem(my_y, near_y)
-    spread_at, note_at, chosen_at = 0, 1, 2
-    grown_at = chosen_at + 1
-    extra_at = grown_at + refs
-    total_at = extra_at + 1
+    far_y = lax.rem(my_y + near_y, count_y)
+    spread_at, note_at, near_at, chosen_at, total_at, cross_at, grown_at = range(7)
+    lane = lax.broadcasted_iota(jnp.int32, (1, half), 1)
 
     def peer(step):
         other = lax.rem(me + step, count)
@@ -71,14 +70,6 @@
 
     def seat_of(device):
         return lax.div(device, count_y) * near_y + lax.rem(lax.rem(device, count_y), near_y)
-
-    barrier = pltpu.get_barrier_semaphore()
-
-    def greet(step, carry):
-        pl.semaphore_signal(barrier, inc=1, device_id=peer(step)[1], device_id_type=MESH)
-        return carry
-
-    lax.fori_loop(1, count, greet, 0)
 
     staged = [
         pltpu.make_async_copy(source, target, stage_sems.at[place])
@@ -90,6 +81,39 @@
     ]
     for copy in staged:
         copy.start()
+
+    barrier = pltpu.get_barrier_semaphore()
+    quarter = count_y // 4
+    early = my_y < near_y
+    late = my_y >= count_y - quarter
+
+    def planes(for_early, for_rest, act, between=None):
+        def at(turn, carry, y):
+            act(lax.rem(my_x + turn, count_x), y)
+            return carry
+
+        for place, (y_early, y_rest) in enumerate(zip(for_early, for_rest)):
+            if between and place == len(for_early) - quarter:
+                between()
+            y = jnp.where(early, y_early, y_rest)
+            pl.when(y != my_y)(functools.partial(act, my_x, y))
+            lax.fori_loop(1, count_x, functools.partial(at, y=y), 0, unroll=count_x <= 8)
+
+    near_first = (
+        *range(near_y, count_y - quarter), *reversed(range(near_y)),
+        *range(count_y - quarter, count_y),
+    )
+    across_first = tuple(range(count_y))
+
+    def tell(semaphore, x, y):
+        pl.semaphore_signal(semaphore, inc=1, device_id=(x, y), device_id_type=MESH)
+
+    def greet(x, y):
+        pl.when(jnp.logical_not(late & (y < near_y)))(
+            functools.partial(tell, barrier, x, y)
+        )
+
+    planes(across_first, across_first, greet)
     staged[0].wait()
 
     row_id, column_id = grid_iota(half, half)
@@ -106,7 +130,7 @@
             start = piece * rows
             source = corner if start < half else mixed
             start = start % half
-            target[piece] = source[start:start + rows]
+            target[piece, :rows, :] = source[start:start + rows]
 
     def factor_of(dimer):
         return jnp.where(live_ref[dimer] > 0, weights_ref[dimer], jnp.float32(0.0))
@@ -119,9 +143,22 @@
         copy.wait()
     note[0:1, :] = diag_row
     for dimer in range(dim_dev):
-        note[dimer + 1:dimer + 2, :] = jnp.full((1, half), factor_of(dimer), F32)
-
-    pl.semaphore_wait(barrier, count - 1)
+        note[dimer + 1:dimer + 2, :] = jnp.where(lane == me, factor_of(dimer), jnp.float32(0.0))
+
+    pl.when(early)(lambda: pl.semaphore_wait(barrier, count - quarter * count_x - 1))
+
+    @pl.when(jnp.logical_not(early))
+    def _():
+        pl.semaphore_wait(barrier, count - 1)
+
+        @pl.when(late)
+        def _():
+            for y in range(near_y):
+                def at(turn, carry, y=y):
+                    tell(ready, lax.rem(my_x + turn, count_x), y)
+                    return carry
+
+                lax.fori_loop(0, count_x, at, 0, unroll=count_x <= 8)
 
     def push(phase, source, target, where_to):
         pltpu.make_async_remote_copy(
@@ -161,10 +198,20 @@
         span = target.at[pl.ds(1, number - 1)]
         pltpu.make_async_copy(span, span, sems.at[phase]).wait()
 
-    to_all(spread_at, lambda other: packed.at[seat_of(other)], held)
-    to_all(note_at, lambda other: note, held_note)
+    def to_desks(act):
+        for y in (0, near_y):
+            pl.when((my_x != 0) | (my_y != y))(functools.partial(act, y))
+
+    def deliver(x, y):
+        other = x * count_y + y
+        push(spread_at, packed.at[seat_of(other)], held.at[wrap(me - other, count)], (x, y))
+
+    to_desks(lambda y: push(note_at, note, held_note.at[wrap(me - y, count)], (0, y)))
+    planes(
+        near_first, across_first, deliver,
+        lambda: pl.when(early)(lambda: pl.semaphore_wait(ready, quarter * count_x)),
+    )
     held[0] = packed[my_seat]
-    held_note[0] = note[...]
 
     for copy in staged[1:4] + staged[6:]:
         copy.wait()
@@ -185,6 +232,36 @@
         return carry
 
     lax.fori_loop(0, count * dim_dev, names, 0)
+
+    at_desk = my_seat == 0
+
+    @pl.when(at_desk)
+    def _():
+        held_note[0] = note[...]
+        drain(recv_sems, note_at, held_note, count)
+
+        def gather(entry, rows):
+            return rows + held_note[entry, 1:, :]
+
+        factors = lax.fori_loop(
+            0, count, gather, jnp.zeros((dim_dev, half), F32), unroll=count <= 32
+        )
+
+        def answer(seat, carry):
+            target = lax.div(seat, near_y) * count_y + first_y + lax.rem(seat, near_y)
+            for ref in range(refs):
+                slot = refs_s[target * refs + ref]
+                notice[seat, ref:ref + 1, :] = held_note[wrap(slot - me, count), 0:1, :]
+            notice[seat, refs:, :] = factors
+            return carry
+
+        lax.fori_loop(0, team, answer, 0, unroll=team <= 32)
+
+        def post(step):
+            push(near_at, notice.at[step], mine, mate(step)[1])
+
+        visit(post, near_y)
+        mine[...] = notice[0]
 
     drain(recv_sems, spread_at, held, count)
 
@@ -250,8 +327,7 @@
         corner = joined[:half, :]
         mixed = joined[half:, :]
         turned = mixed.T
-        slot = refs_s[me * refs + ref]
-        diag_row = held_note[wrap(slot - me, count), 0:1, :]
+        diag_row = mine[ref:ref + 1, :]
         start = side * width
         mid = start + half
         end = start + width
@@ -263,14 +339,44 @@
             jnp.where(on_diag, diag_row, jnp.where(strict, mixed, turned)),
         )
 
-    def emit(ref, block):
+    def grown(ref):
+        return (grown_second if ref % 2 else grown_first).at[ref // 2]
+
+    def landed(ref):
+        return (landed_second if ref % 2 else landed_first).at[ref // 2]
+
+    def emit(ref, block, other_row):
         corner, mixed, diag_row = pack(block[:half, :half], block[:half, half:], block[half:, half:])
-        scatter_rows(grown.at[ref], corner, mixed)
-        extra[ref:ref + 1, :] = diag_row
-        to_team(grown_at + ref, lambda other: grown.at[ref, seat_of(other)], landed.at[ref])
+        scatter_rows(grown(ref), corner, mixed)
+        if ref % 2:
+            for piece in range(team):
+                grown(ref)[piece, rows:rows + 1, :] = other_row
+                grown(ref)[piece, rows + 1:rows + 2, :] = diag_row
+        to_team(grown_at + ref, lambda other: grown(ref).at[seat_of(other)], landed(ref))
+        return diag_row
 
     couple(0)
-    drain(recv_sems, note_at, held_note, count)
+    def count_hits(device, hits):
+        for dimer in range(dim_dev):
+            first = (device * dim_dev + dimer) * 2
+            named_me = (refs_s[first] == me) | (refs_s[first + 1] == me)
+            hit = jnp.where(named_me, 1.0, 0.0).astype(F32)
+            hits = tuple(
+                jnp.where(lane == device, hit, row) if place == dimer else row
+                for place, row in enumerate(hits)
+            )
+        return hits
+
+    hits = lax.fori_loop(
+        0, count, count_hits, (jnp.zeros((1, half), F32),) * dim_dev, unroll=count <= 32
+    )
+    pl.when(jnp.logical_not(at_desk))(
+        lambda: pltpu.make_async_copy(mine, mine, recv_sems.at[near_at]).wait()
+    )
+    scale = jnp.ones((1, 1), F32)
+    for dimer in range(dim_dev):
+        row = hits[dimer] * mine[refs + dimer:refs + dimer + 1, :]
+        scale = scale + jnp.sum(row, axis=1, keepdims=True)
     drain(recv_sems, chosen_at, got, team)
 
     for dimer in range(dim_dev):
@@ -296,26 +402,24 @@
             keep(top, low, times(m_pair, top, every, m_pair, low))
             if repeat < ITERS - 2:
                 keep(low, low, times(m_pair, low, every, m_pair, low))
-        emit(first, factor * (
+        first_row = emit(first, factor * (
             3.0 * square[top, top] - 2.0 * times(q_pair, top, every, m_pair, top)
-        ))
+        ), None)
         keep(low, low, times(m_pair, low, every, m_pair, low))
         emit(second, factor * (
             3.0 * square[low, low] - 2.0 * times(m_pair, low, every, q_pair, low)
-        ))
-
-    to_all(extra_at, lambda other: extra, landed_extra)
+        ), first_row)
+
     for ref in range(refs):
-        landed[ref, 0] = grown[ref, my_seat]
-    landed_extra[0] = extra[...]
+        landed(ref)[0] = grown(ref)[my_seat]
 
     for ref in range(refs):
-        drain(recv_sems, grown_at + ref, landed.at[ref], team)
+        drain(recv_sems, grown_at + ref, landed(ref), team)
         if rows % 8 == 0:
-            values = landed[ref].reshape(span, half)
+            values = landed(ref)[:, :rows, :].reshape(span, half)
         else:
             for entry in range(team):
-                flat[entry * rows:(entry + 1) * rows, :] = landed[ref, entry]
+                flat[entry * rows:(entry + 1) * rows, :] = landed(ref)[entry, :rows, :]
             values = flat[...]
         gained = mm(table[:, ref * span:(ref + 1) * span], jnp.concatenate(split(values), axis=1))
         gained = gained[:, :half] + gained[:, half:]
@@ -325,23 +429,22 @@
     to_all(total_at, lambda other: totals.at[other], back)
     back[0] = totals[me]
 
-    drain(recv_sems, extra_at, landed_extra, count)
-
-    def collect(entry, carry):
-        source = lax.rem(me + entry, count)
-        diag_total, scale = carry
+    def collect(entry, sums):
+        source = mate(entry)[0]
         for ref in range(refs):
-            hit = jnp.where(refs_s[source * refs + ref] == me, 1, 0)
-            mask = jnp.full((1, half), hit, jnp.int32) > 0
-            diag_total = diag_total + jnp.where(mask, landed_extra[entry, ref:ref + 1, :], 0.0)
-            row = 1 + ref // 2
-            scale = scale + jnp.where(mask, held_note[entry, row:row + 1, :], 0.0)
-        return diag_total, scale
-
-    diag_total, scale = lax.fori_loop(
-        0, count, collect, (jnp.zeros((1, half), F32), jnp.ones((1, half), F32)),
-        unroll=count <= 32,
-    )
+            row = landed(ref | 1)[entry, rows + ref % 2:rows + ref % 2 + 1, :]
+            named_at = refs_s[source * refs + ref]
+            sums = tuple(
+                total + jnp.where(jnp.full((1, half), named_at, jnp.int32) == owner, row, 0.0)
+                for owner, total in zip((my_x * count_y + far_y, me), sums)
+            )
+        return sums
+
+    cross_row, own_row = lax.fori_loop(
+        0, team, collect, (jnp.zeros((1, half), F32),) * 2, unroll=team <= 32
+    )
+    cross[...] = cross_row
+    push(cross_at, cross, crossed, (my_x, far_y))
 
     drain(recv_sems, total_at, back, count)
     for piece in range(team):
@@ -349,6 +452,8 @@
         joined[piece * rows:(piece + 1) * rows, :] = (
             back[wrap(source - me, count)] + back[wrap(source + near_y - me, count)]
         )
+    pltpu.make_async_copy(crossed, crossed, recv_sems.at[cross_at]).wait()
+    diag_total = own_row + crossed[...]
     corner = joined[:half, :]
     mixed = joined[half:, :]
     turned = mixed.T
@@ -363,12 +468,13 @@
     ) / scale
 
     drain(send_sems, spread_at, held, count)
-    drain(send_sems, note_at, held_note, count)
+    to_desks(lambda y: pltpu.make_async_copy(note, note, send_sems.at[note_at]).wait())
+    pl.when(at_desk)(lambda: drain(send_sems, near_at, notice, team))
     drain(send_sems, chosen_at, got, team)
     for ref in range(refs):
-        drain(send_sems, grown_at + ref, landed.at[ref], team)
-    drain(send_sems, extra_at, landed_extra, count)
+        drain(send_sems, grown_at + ref, grown(ref), team)
     drain(send_sems, total_at, back, count)
+    pltpu.make_async_copy(cross, cross, send_sems.at[cross_at]).wait()
 
 
 def solution(mesh):
@@ -382,13 +488,13 @@
         half = width // 2
         team = count // 2
         rows = width // team
-        assert frag_dev == 1 and rows * team == width and count_y % 2 == 0
+        assert frag_dev == 1 and rows * team == width and count_y % 4 == 0 and count <= half
         vmem = lambda *shape: pltpu.VMEM(shape, F32)
         bf16 = lambda *shape: pltpu.VMEM(shape, BF16)
         in_vmem = pl.BlockSpec(memory_space=pltpu.VMEM)
         smem = lambda array: pltpu.SMEM(array.shape, array.dtype)
         pairs = dimer_pairs.T
-        phases = 5 + refs
+        phases = 6 + refs
         return pl.pallas_call(
             functools.partial(kernel, count_x, count_y),
             out_shape=pltpu.VMEM(density.shape, F32),
@@ -408,6 +514,8 @@
                 vmem(count, rows, half),
                 vmem(1 + dim_dev, half),
                 vmem(count, 1 + dim_dev, half),
+                vmem(team, refs + dim_dev, half),
+                vmem(refs + dim_dev, half),
                 vmem(team, refs, rows, half),
                 vmem(team, refs, rows, half),
                 vmem(width, half),
@@ -416,17 +524,20 @@
                 bf16(2 * width, 2 * width),
                 bf16(2 * width, 2 * width),
                 vmem(2 * width, 2 * width),
-                vmem(refs, team, rows, half),
-                vmem(refs, team, rows, half),
-                vmem(refs, half),
-                vmem(count, refs, half),
+                vmem(dim_dev, team, rows, half),
+                vmem(dim_dev, team, rows + 2, half),
+                vmem(dim_dev, team, rows, half),
+                vmem(dim_dev, team, rows + 2, half),
                 vmem(team * rows if rows % 8 else 8, half),
                 bf16(count * rows, refs * team * rows),
                 vmem(count, rows, half),
                 vmem(count, rows, half),
+                vmem(1, half),
+                vmem(1, half),
                 pltpu.SemaphoreType.DMA((phases,)),
                 pltpu.SemaphoreType.DMA((phases,)),
                 pltpu.SemaphoreType.DMA((7,)),
+                pltpu.SemaphoreType.REGULAR,
             ],
             compiler_params=pltpu.CompilerParams(collective_id=0, has_side_effects=True),
         )(density, coupling, weights, live_mask, pairs, dimer_slot, frag_slot)

time: 40.1 us -> 38.9 us (0.970)
  Pallas kernels: 37.9 us -> 36.7 us
    pallas_call x1, Pallas kernels: 37.9 us -> 36.7 us  [per_device(): pl.pallas_call(functools.partial(kernel, count_x, count_y), out_shape=plt...]
where the time goes in v2:
time: 38.9 us; the launch traced here: 38.7 us
  Pallas kernels  36.7 us (94%)
  between operations  1.3 us (3%)
  local copies, waits for them, and re-layouts  0.71 us (2%)
    pallas_call x1, Pallas kernels, per_device(): pl.pallas_call(functools.partial(kernel, count_x, count_y), out_shape=plt...  36.7 us

profile of v2, /device:TPU:0, one launch (start us, length us, event | category | flops | bytes accessed | tf_op | source)
XLA Modules:
  0.0 38.7 jit_solution(6020094661814750826)
XLA Ops:
  1.3 36.7 %shard_map.73 = f32[1,256,256]{2,1,0:T(8,128)S(1)} custom-call(f32[1,256,256]{2,1,0:T(8,128)} %density_in.1, f32[1,256,256]{2,1,0:T(8,128)} %coupling_in.1, f32[1]{0:T(128)S(6)} %copy.10.weights_in, s32[1]{0:T(128)S(6)} %copy.11.live_in, s32[2,32]{1,0:T(2,128)} %bitcast.1, s32[32]{0:T(128)} %dslot_in.1, s32[32]{0:T(128)} %fslot_in.1), custom_call_target="tpu_custom_call" | custom-call | tf_op jit(solution)/shard_map/pallas_call | solution.py:498
  38.0 0.7 %copy.9 = f32[1,256,256]{2,1,0:T(8,128)} copy(f32[1,256,256]{2,1,0:T(8,128)S(1)} %shard_map.73) | data formatting | bytes 524288

commit v3 on v2

--- a/solution.py
+++ b/solution.py
@@ -59,10 +59,6 @@
     spread_at, note_at, near_at, chosen_at, total_at, cross_at, grown_at = range(7)
     lane = lax.broadcasted_iota(jnp.int32, (1, half), 1)
 
-    def peer(step):
-        other = lax.rem(me + step, count)
-        return other, (lax.div(other, count_y), lax.rem(other, count_y))
-
     def mate(step):
         seat = lax.rem(my_seat + step, team)
         x, y = lax.div(seat, near_y), first_y + lax.rem(seat, near_y)
@@ -87,29 +83,41 @@
     early = my_y < near_y
     late = my_y >= count_y - quarter
 
+    def column(turn):
+        x, bit = my_x, 1
+        while bit < count_x:
+            toggle = bit - 2 * bit * lax.rem(lax.div(my_x, bit), 2)
+            x = x + lax.rem(lax.div(count_x - 1 - turn, bit), 2) * toggle
+            bit *= 2
+        return x
+
+    def plane(y, act):
+        def at(turn, carry):
+            act(column(turn), y)
+            return carry
+
+        lax.fori_loop(0, count_x - 1, at, 0, unroll=count_x <= 8)
+        pl.when(y != my_y)(functools.partial(act, my_x, y))
+
     def planes(for_early, for_rest, act, between=None):
-        def at(turn, carry, y):
-            act(lax.rem(my_x + turn, count_x), y)
-            return carry
-
         for place, (y_early, y_rest) in enumerate(zip(for_early, for_rest)):
             if between and place == len(for_early) - quarter:
                 between()
-            y = jnp.where(early, y_early, y_rest)
-            pl.when(y != my_y)(functools.partial(act, my_x, y))
-            lax.fori_loop(1, count_x, functools.partial(at, y=y), 0, unroll=count_x <= 8)
+            plane(jnp.where(early, y_early, y_rest), act)
 
     near_first = (
         *range(near_y, count_y - quarter), *reversed(range(near_y)),
         *range(count_y - quarter, count_y),
     )
     across_first = tuple(range(count_y))
+    far_first = sorted(range(count_y), key=lambda y: -abs(y - near_y + 1))
+    far_first_rest = [count_y - 1 - y for y in far_first]
 
     def tell(semaphore, x, y):
         pl.semaphore_signal(semaphore, inc=1, device_id=(x, y), device_id_type=MESH)
 
     def greet(x, y):
-        pl.when(jnp.logical_not(late & (y < near_y)))(
+        pl.when(jnp.logical_not(late) | (y >= count_y - quarter))(
             functools.partial(tell, barrier, x, y)
         )
 
@@ -145,20 +153,15 @@
     for dimer in range(dim_dev):
         note[dimer + 1:dimer + 2, :] = jnp.where(lane == me, factor_of(dimer), jnp.float32(0.0))
 
-    pl.when(early)(lambda: pl.semaphore_wait(barrier, count - quarter * count_x - 1))
-
-    @pl.when(jnp.logical_not(early))
+    pl.when(jnp.logical_not(late))(
+        lambda: pl.semaphore_wait(barrier, count - quarter * count_x - 1)
+    )
+
+    @pl.when(late)
     def _():
         pl.semaphore_wait(barrier, count - 1)
-
-        @pl.when(late)
-        def _():
-            for y in range(near_y):
-                def at(turn, carry, y=y):
-                    tell(ready, lax.rem(my_x + turn, count_x), y)
-                    return carry
-
-                lax.fori_loop(0, count_x, at, 0, unroll=count_x <= 8)
+        for y in range(count_y - quarter):
+            plane(jnp.int32(y), functools.partial(tell, ready))
 
     def push(phase, source, target, where_to):
         pltpu.make_async_remote_copy(
@@ -170,29 +173,23 @@
             device_id_type=MESH,
         ).start()
 
-    def visit(act, cycle):
-        def at(turn, carry, lag):
-            act(turn * cycle + lag)
-            return carry
-
-        for lag in sorted(range(cycle), key=lambda lag: -min(lag, cycle - lag)):
-            lax.fori_loop(
-                0 if lag else 1, count_x, functools.partial(at, lag=lag), 0, unroll=count_x <= 8
-            )
-
     def to_all(phase, piece_for, target):
-        def act(step):
-            other, where_to = peer(step)
-            push(phase, piece_for(other), target.at[count - step], where_to)
-
-        visit(act, count_y)
+        def act(x, y):
+            other = x * count_y + y
+            push(phase, piece_for(other), target.at[wrap(me - other, count)], (x, y))
+
+        planes(far_first, far_first_rest, act)
+
+    def team_planes(act):
+        for lag in range(1, near_y + 1):
+            plane(first_y + lax.rem(my_y - first_y + lag, near_y), act)
 
     def to_team(phase, piece_for, target):
-        def act(step):
-            other, where_to = mate(step)
-            push(phase, piece_for(other), target.at[team - step], where_to)
-
-        visit(act, near_y)
+        def act(x, y):
+            seat = seat_of(x * count_y + y)
+            push(phase, piece_for(seat), target.at[wrap(my_seat - seat, team)], (x, y))
+
+        team_planes(act)
 
     def drain(sems, phase, target, number):
         span = target.at[pl.ds(1, number - 1)]
@@ -209,7 +206,9 @@
     to_desks(lambda y: push(note_at, note, held_note.at[wrap(me - y, count)], (0, y)))
     planes(
         near_first, across_first, deliver,
-        lambda: pl.when(early)(lambda: pl.semaphore_wait(ready, quarter * count_x)),
+        lambda: pl.when(jnp.logical_not(late))(
+            lambda: pl.semaphore_wait(ready, quarter * count_x)
+        ),
     )
     held[0] = packed[my_seat]
 
@@ -257,10 +256,10 @@
 
         lax.fori_loop(0, team, answer, 0, unroll=team <= 32)
 
-        def post(step):
-            push(near_at, notice.at[step], mine, mate(step)[1])
-
-        visit(post, near_y)
+        def post(x, y):
+            push(near_at, notice.at[seat_of(x * count_y + y)], mine, (x, y))
+
+        team_planes(post)
         mine[...] = notice[0]
 
     drain(recv_sems, spread_at, held, count)
@@ -273,7 +272,7 @@
         return carry
 
     lax.fori_loop(0, team, choose, 0, unroll=team <= 32)
-    to_team(chosen_at, lambda other: chosen.at[seat_of(other)], got)
+    to_team(chosen_at, lambda seat: chosen.at[seat], got)
     got[0] = chosen[my_seat]
 
     span = team * rows
@@ -352,7 +351,7 @@
             for piece in range(team):
                 grown(ref)[piece, rows:rows + 1, :] = other_row
                 grown(ref)[piece, rows + 1:rows + 2, :] = diag_row
-        to_team(grown_at + ref, lambda other: grown(ref).at[seat_of(other)], landed(ref))
+        to_team(grown_at + ref, lambda seat: grown(ref).at[seat], landed(ref))
         return diag_row
 
     couple(0)
@@ -489,6 +488,7 @@
         team = count // 2
         rows = width // team
         assert frag_dev == 1 and rows * team == width and count_y % 4 == 0 and count <= half
+        assert count_x & (count_x - 1) == 0
         vmem = lambda *shape: pltpu.VMEM(shape, F32)
         bf16 = lambda *shape: pltpu.VMEM(shape, BF16)
         in_vmem = pl.BlockSpec(memory_space=pltpu.VMEM)

time: 38.9 us -> 37.8 us (0.972)
  Pallas kernels: 36.7 us -> 35.6 us
    pallas_call x1, Pallas kernels: 36.7 us -> 35.6 us  [per_device(): pl.pallas_call(functools.partial(kernel, count_x, count_y), out_shape=plt...]
where the time goes in v3:
time: 37.8 us; the launch traced here: 37.6 us
  Pallas kernels  35.6 us (94%)
  between operations  1.3 us (3%)
  local copies, waits for them, and re-layouts  0.71 us (2%)
    pallas_call x1, Pallas kernels, per_device(): pl.pallas_call(functools.partial(kernel, count_x, count_y), out_shape=plt...  35.6 us

profile of v3, /device:TPU:0, one launch (start us, length us, event | category | flops | bytes accessed | tf_op | source)
XLA Modules:
  0.0 37.6 jit_solution(14068691201159110647)
XLA Ops:
  1.3 35.6 %shard_map.73 = f32[1,256,256]{2,1,0:T(8,128)S(1)} custom-call(f32[1,256,256]{2,1,0:T(8,128)} %density_in.1, f32[1,256,256]{2,1,0:T(8,128)} %coupling_in.1, f32[1]{0:T(128)S(6)} %copy.10.weights_in, s32[1]{0:T(128)S(6)} %copy.11.live_in, s32[2,32]{1,0:T(2,128)} %bitcast.1, s32[32]{0:T(128)} %dslot_in.1, s32[32]{0:T(128)} %fslot_in.1), custom_call_target="tpu_custom_call" | custom-call | tf_op jit(solution)/shard_map/pallas_call | solution.py:498
  36.9 0.7 %copy.9 = f32[1,256,256]{2,1,0:T(8,128)} copy(f32[1,256,256]{2,1,0:T(8,128)S(1)} %shard_map.73) | data formatting | bytes 524288

commit v4 on v3

--- a/solution.py
+++ b/solution.py
@@ -110,9 +110,6 @@
         *range(count_y - quarter, count_y),
     )
     across_first = tuple(range(count_y))
-    far_first = sorted(range(count_y), key=lambda y: -abs(y - near_y + 1))
-    far_first_rest = [count_y - 1 - y for y in far_first]
-
     def tell(semaphore, x, y):
         pl.semaphore_signal(semaphore, inc=1, device_id=(x, y), device_id_type=MESH)
 
@@ -173,13 +170,6 @@
             device_id_type=MESH,
         ).start()
 
-    def to_all(phase, piece_for, target):
-        def act(x, y):
-            other = x * count_y + y
-            push(phase, piece_for(other), target.at[wrap(me - other, count)], (x, y))
-
-        planes(far_first, far_first_rest, act)
-
     def team_planes(act):
         for lag in range(1, near_y + 1):
             plane(first_y + lax.rem(my_y - first_y + lag, near_y), act)
@@ -280,10 +270,14 @@
     lane_id = lax.broadcasted_iota(jnp.int32, (1, lanes), 1)
     lane_entry = lane_id // rows
 
+    def owner_row(device):
+        y = lax.rem(lax.rem(device, count_y) + count_y + near_y - first_y, count_y)
+        return y * count_x + lax.div(device, count_y)
+
     def spread(entry, row):
         ref = lax.div(entry, team)
         source = mate(lax.rem(entry, team))[0]
-        return jnp.where(lane_entry == entry, refs_s[source * refs + ref], row)
+        return jnp.where(lane_entry == entry, owner_row(refs_s[source * refs + ref]), row)
 
     named = lax.fori_loop(
         0, team * refs, spread, jnp.zeros((1, lanes), jnp.int32), unroll=team * refs <= 64
@@ -401,10 +395,10 @@
             keep(top, low, times(m_pair, top, every, m_pair, low))
             if repeat < ITERS - 2:
                 keep(low, low, times(m_pair, low, every, m_pair, low))
+        keep(low, low, times(m_pair, low, every, m_pair, low))
         first_row = emit(first, factor * (
             3.0 * square[top, top] - 2.0 * times(q_pair, top, every, m_pair, top)
         ), None)
-        keep(low, low, times(m_pair, low, every, m_pair, low))
         emit(second, factor * (
             3.0 * square[low, low] - 2.0 * times(m_pair, low, every, q_pair, low)
         ), first_row)
@@ -412,6 +406,12 @@
     for ref in range(refs):
         landed(ref)[0] = grown(ref)[my_seat]
 
+    def gain(ref, values, start, stop):
+        block = table[start * rows:stop * rows, ref * span:(ref + 1) * span]
+        gained = mm(block, values)
+        return gained[:, :half] + gained[:, half:]
+
+    sums = []
     for ref in range(refs):
         drain(recv_sems, grown_at + ref, landed(ref), team)
         if rows % 8 == 0:
@@ -420,13 +420,27 @@
             for entry in range(team):
                 flat[entry * rows:(entry + 1) * rows, :] = landed(ref)[entry, :rows, :]
             values = flat[...]
-        gained = mm(table[:, ref * span:(ref + 1) * span], jnp.concatenate(split(values), axis=1))
-        gained = gained[:, :half] + gained[:, half:]
-        sums = gained if ref == 0 else sums + gained
-    for piece in range(count):
-        totals[piece] = sums[piece * rows:(piece + 1) * rows, :]
-    to_all(total_at, lambda other: totals.at[other], back)
-    back[0] = totals[me]
+        values = jnp.concatenate(split(values), axis=1)
+        if ref < refs - 1:
+            added = [gain(ref, values, start, start + team) for start in (0, team)]
+            sums = [a + b for a, b in zip(sums, added)] if sums else added
+
+    def deal(side):
+        start = side * team
+        whole = sums[side] + gain(refs - 1, values, start, start + team)
+        for piece in range(team):
+            totals[start + piece] = whole[piece * rows:(piece + 1) * rows, :]
+
+    def hand(x, y):
+        other = x * count_y + y
+        push(total_at, totals.at[owner_row(other)], back.at[wrap(me - other, count)], (x, y))
+
+    deal(0)
+    for lag in range(near_y):
+        plane(jnp.where(early, count_y - 1 - lag, lag), hand)
+    deal(1)
+    team_planes(hand)
+    back[0] = totals[owner_row(me)]
 
     def collect(entry, sums):
         source = mate(entry)[0]

time: 37.8 us -> 37.7 us (level)
  no operation moved by 1% of the time
where the time goes in v4:
time: 37.7 us; the launch traced here: 37.6 us
  Pallas kernels  35.6 us (94%)
  between operations  1.3 us (3%)
  local copies, waits for them, and re-layouts  0.71 us (2%)
    pallas_call x1, Pallas kernels, per_device(): pl.pallas_call(functools.partial(kernel, count_x, count_y), out_shape=plt...  35.6 us

profile of v4, /device:TPU:0, one launch (start us, length us, event | category | flops | bytes accessed | tf_op | source)
XLA Modules:
  0.0 37.6 jit_solution(9643434413805744336)
XLA Ops:
  1.3 35.6 %shard_map.73 = f32[1,256,256]{2,1,0:T(8,128)S(1)} custom-call(f32[1,256,256]{2,1,0:T(8,128)} %density_in.1, f32[1,256,256]{2,1,0:T(8,128)} %coupling_in.1, f32[1]{0:T(128)S(6)} %copy.10.weights_in, s32[1]{0:T(128)S(6)} %copy.11.live_in, s32[2,32]{1,0:T(2,128)} %bitcast.1, s32[32]{0:T(128)} %dslot_in.1, s32[32]{0:T(128)} %fslot_in.1), custom_call_target="tpu_custom_call" | custom-call | tf_op jit(solution)/shard_map/pallas_call | solution.py:512
  36.9 0.7 %copy.9 = f32[1,256,256]{2,1,0:T(8,128)} copy(f32[1,256,256]{2,1,0:T(8,128)S(1)} %shard_map.73) | data formatting | bytes 524288

commit v5 on v4

--- a/solution.py
+++ b/solution.py
@@ -106,7 +106,7 @@
             plane(jnp.where(early, y_early, y_rest), act)
 
     near_first = (
-        *range(near_y, count_y - quarter), *reversed(range(near_y)),
+        *range(near_y, count_y - quarter), *range(near_y),
         *range(count_y - quarter, count_y),
     )
     across_first = tuple(range(count_y))

time: 37.7 us -> 37.7 us (level)
  no operation moved by 1% of the time
where the time goes in v5:
time: 37.7 us; the launch traced here: 37.6 us
  Pallas kernels  35.6 us (94%)
  between operations  1.3 us (3%)
  local copies, waits for them, and re-layouts  0.71 us (2%)
    pallas_call x1, Pallas kernels, per_device(): pl.pallas_call(functools.partial(kernel, count_x, count_y), out_shape=plt...  35.6 us

profile of v5, /device:TPU:0, one launch (start us, length us, event | category | flops | bytes accessed | tf_op | source)
XLA Modules:
  0.0 37.6 jit_solution(3739317851054545497)
XLA Ops:
  1.3 35.6 %shard_map.73 = f32[1,256,256]{2,1,0:T(8,128)S(1)} custom-call(f32[1,256,256]{2,1,0:T(8,128)} %density_in.1, f32[1,256,256]{2,1,0:T(8,128)} %coupling_in.1, f32[1]{0:T(128)S(6)} %copy.10.weights_in, s32[1]{0:T(128)S(6)} %copy.11.live_in, s32[2,32]{1,0:T(2,128)} %bitcast.1, s32[32]{0:T(128)} %dslot_in.1, s32[32]{0:T(128)} %fslot_in.1), custom_call_target="tpu_custom_call" | custom-call | tf_op jit(solution)/shard_map/pallas_call | solution.py:512
  36.9 0.7 %copy.9 = f32[1,256,256]{2,1,0:T(8,128)} copy(f32[1,256,256]{2,1,0:T(8,128)S(1)} %shard_map.73) | data formatting | bytes 524288
